TPU v7x, 32 devices: a whole 2x2x4 slice. The times are simulated.
32 devices in a mesh: sweep: 1, dp: 8 (over z, y), tensor: 4 (over x, core).
Axes of the slice: x: 2, y: 2, z: 4, core: 2. Of those that a mesh axis runs over, the one named last changes fastest.
Arguments:
- checkpoint: bfloat16 [1024, 8192], P(('sweep', 'dp'), 'tensor'), may hold values from -6 to 6
- norm_gain: bfloat16 [8192], P(('sweep', 'tensor')), may hold values from 0.5 to 1.5
- w_query: bfloat16 [8192, 4096], P(('sweep', 'dp'), 'tensor'), may hold values from -1 to 1
- w_key: bfloat16 [8192, 512], P(('sweep', 'dp'), 'tensor'), may hold values from -8 to 8
- w_value: bfloat16 [8192, 512], P(('sweep', 'dp'), 'tensor'), may hold values from -0.0625 to 0.0625
- grad_attn: bfloat16 [1024, 4096], P(('sweep', 'dp'), 'tensor'), may hold values from -6 to 6
Outputs:
- d_checkpoint: bfloat16 [1024, 8192], P(('sweep', 'dp'), 'tensor')
- grad_gain: float32 [8192], P(('sweep', 'tensor'))
- grad_query: float32 [8192, 4096], P(('sweep', 'dp'), 'tensor')
- grad_key: float32 [8192, 512], P(('sweep', 'dp'), 'tensor')
- grad_value: float32 [8192, 512], P(('sweep', 'dp'), 'tensor')
All inputs are finite; a program needn't handle non-finite values.
Results may differ from a plain program's by a relative error of at most 0.025.
The roundings to bfloat16 on the way count: a program that leaves them out, or rounds other values in their place, can miss the bound.
Values may be sent and summed in bfloat16 or wider, within the bound.
No kernel may reach another device: no remote copies, remote signals or barrier semaphores. Data moves between devices by JAX's collectives and lax.ppermute only.
A program may use at most 128 MiB of HBM per device.

v0:
```python
import jax
import jax.numpy as jnp
from jax import lax
from jax.sharding import PartitionSpec as P

QHEADS = 32
KVHEADS = 4
HD = 128
EPS = 1e-05
THETA = 500000.0


def round_half(field):
    return lax.optimization_barrier(field.astype(jnp.bfloat16))


def angles(positions, head_width):
    frequency = THETA ** (-(jnp.arange(head_width // 2, dtype=jnp.float32) * 2.0) / head_width)
    turned = positions.astype(jnp.float32)[:, None] * frequency[None, :]
    return (jnp.cos(turned)[:, None, :], jnp.sin(turned)[:, None, :])


def rotate(field, cosine_table, sine_table):
    half_width = field.shape[-1] // 2
    front_half = field[..., :half_width]
    back_half = field[..., half_width:]
    return jnp.concatenate(
        [
            front_half * cosine_table - back_half * sine_table,
            back_half * cosine_table + front_half * sine_table,
        ],
        -1,
    )


def rotate_back(field, cosine_table, sine_table):
    half_width = field.shape[-1] // 2
    front_half = field[..., :half_width]
    back_half = field[..., half_width:]
    return jnp.concatenate(
        [
            front_half * cosine_table + back_half * sine_table,
            back_half * cosine_table - front_half * sine_table,
        ],
        -1,
    )


def project_back(grads, matrix):
    return jnp.einsum("tc,dc->td", grads, matrix, preferred_element_type=jnp.float32)


def on_device(checkpoint, norm_gain, w_query, w_key, w_value, grad_attn):
    row_count = checkpoint.shape[0]
    head_width = HD
    group_size = QHEADS // KVHEADS
    full_x, full_gain = (
        lax.all_gather(checkpoint, "tensor", axis=1, tiled=True),
        lax.all_gather(norm_gain, "tensor", axis=0, tiled=True),
    )
    x_wide = full_x.astype(jnp.float32)
    gain_wide = full_gain.astype(jnp.float32)
    model_width = full_x.shape[1]
    inverse = lax.rsqrt(jnp.mean(x_wide * x_wide, -1, keepdims=True) + EPS)
    normed = (x_wide * inverse * gain_wide).astype(jnp.bfloat16)
    query_all, key_all, value_all = (
        lax.all_gather(w_query, "dp", axis=0, tiled=True),
        lax.all_gather(w_key, "dp", axis=0, tiled=True),
        lax.all_gather(w_value, "dp", axis=0, tiled=True),
    )
    q_heads = query_all.shape[1] // head_width
    own_kv = max(1, q_heads // group_size)
    run_heads = q_heads // own_kv
    first_kv = lax.axis_index("tensor") * q_heads // group_size
    queries = jnp.dot(normed, query_all, preferred_element_type=jnp.float32).reshape(
        row_count, q_heads, head_width
    )
    key_local = jnp.dot(normed, key_all, preferred_element_type=jnp.float32)
    value_local = jnp.dot(normed, value_all, preferred_element_type=jnp.float32)
    key_cols_all, value_cols_all = (
        lax.all_gather(key_local, "tensor", axis=1, tiled=True),
        lax.all_gather(value_local, "tensor", axis=1, tiled=True),
    )
    kv_total = key_cols_all.shape[1] // head_width
    first_row = lax.axis_index("dp") * row_count
    own_positions = first_row + jnp.arange(row_count, dtype=jnp.int32)
    cosine_table, sine_table = angles(own_positions, head_width)
    query_rot = rotate(queries, cosine_table, sine_table).astype(jnp.bfloat16)
    key_heads = lax.dynamic_slice_in_dim(
        key_cols_all.reshape(row_count, head_width, kv_total), first_kv, own_kv, 2
    )
    value_heads = lax.dynamic_slice_in_dim(
        value_cols_all.reshape(row_count, head_width, kv_total), first_kv, own_kv, 2
    )
    key_turned = rotate(jnp.transpose(key_heads, (0, 2, 1)), cosine_table, sine_table)
    key_rot = key_turned.astype(jnp.bfloat16).reshape(row_count, own_kv * head_width)
    value_half = (
        jnp.transpose(value_heads, (0, 2, 1))
        .astype(jnp.bfloat16)
        .reshape(row_count, own_kv * head_width)
    )
    gathered_keys, gathered_values = (
        lax.all_gather(key_rot, "dp", axis=0, tiled=True),
        lax.all_gather(value_half, "dp", axis=0, tiled=True),
    )
    seq_length = gathered_keys.shape[0]
    keys_three = gathered_keys.reshape(seq_length, own_kv, head_width)
    values_three = gathered_values.reshape(seq_length, own_kv, head_width)
    score_scale = head_width ** (-0.5)
    query_grp = query_rot.reshape(row_count, own_kv, run_heads, head_width)
    upstream = grad_attn.reshape(row_count, own_kv, run_heads, head_width)
    scores = (
        jnp.einsum("tkgd,skd->kgts", query_grp, keys_three, preferred_element_type=jnp.float32)
        * score_scale
    )
    allowed = own_positions[:, None] >= jnp.arange(seq_length, dtype=jnp.int32)[None, :]
    scores = jnp.where(allowed, scores, -jnp.inf)
    row_top = jnp.max(scores, -1, keepdims=True)
    raw_weights = jnp.exp(scores - row_top)
    chances = raw_weights / jnp.sum(raw_weights, -1, keepdims=True)
    chances_half = chances.astype(jnp.bfloat16)
    attended = jnp.einsum(
        "kgts,skd->tkgd", chances_half, values_three, preferred_element_type=jnp.float32
    )
    row_delta = jnp.sum(upstream.astype(jnp.float32) * attended, -1)
    prob_grads = jnp.einsum(
        "tkgd,skd->kgts", upstream, values_three, preferred_element_type=jnp.float32
    )
    dscore = chances * (prob_grads - jnp.transpose(row_delta, (1, 2, 0))[..., None])
    dscore_half = dscore.astype(jnp.bfloat16)
    dquery = (
        jnp.einsum("kgts,skd->tkgd", dscore_half, keys_three, preferred_element_type=jnp.float32)
        * score_scale
    )
    dkey_part = (
        jnp.einsum("kgts,tkgd->skd", dscore_half, query_grp, preferred_element_type=jnp.float32)
        * score_scale
    )
    dvalue_part = jnp.einsum(
        "kgts,tkgd->skd", chances_half, upstream, preferred_element_type=jnp.float32
    )
    dkey_sum, dvalue_sum = (
        lax.psum_scatter(
            dkey_part.reshape(seq_length, own_kv * head_width).astype(jnp.bfloat16),
            "dp",
            scatter_dimension=0,
            tiled=True,
        ).astype(jnp.float32),
        lax.psum_scatter(
            dvalue_part.reshape(seq_length, own_kv * head_width).astype(jnp.bfloat16),
            "dp",
            scatter_dimension=0,
            tiled=True,
        ).astype(jnp.float32),
    )
    dkey_back = rotate_back(
        dkey_sum.reshape(row_count, own_kv, head_width), cosine_table, sine_table
    )
    dvalue_back = dvalue_sum.reshape(row_count, own_kv, head_width)
    empty_heads = jnp.zeros((row_count, kv_total, head_width), jnp.float32)
    zero_start = jnp.zeros((), jnp.int32)
    dkey_embed = lax.dynamic_update_slice(
        empty_heads, dkey_back, (zero_start, first_kv, zero_start)
    )
    dvalue_embed = lax.dynamic_update_slice(
        empty_heads, dvalue_back, (zero_start, first_kv, zero_start)
    )
    dkey_embed = jnp.transpose(dkey_embed, (0, 2, 1)).reshape(row_count, head_width * kv_total)
    dvalue_embed = jnp.transpose(dvalue_embed, (0, 2, 1)).reshape(row_count, head_width * kv_total)
    dkey_cols, dvalue_cols = (
        lax.psum_scatter(
            dkey_embed.astype(jnp.bfloat16), "tensor", scatter_dimension=1, tiled=True
        ).astype(jnp.float32),
        lax.psum_scatter(
            dvalue_embed.astype(jnp.bfloat16), "tensor", scatter_dimension=1, tiled=True
        ).astype(jnp.float32),
    )
    dquery_pre = (
        rotate_back(dquery.reshape(row_count, q_heads, head_width), cosine_table, sine_table)
        .astype(jnp.bfloat16)
        .reshape(row_count, q_heads * head_width)
    )
    dkey_pre = dkey_cols.astype(jnp.bfloat16)
    dvalue_pre = dvalue_cols.astype(jnp.bfloat16)
    partial_input = (
        project_back(dquery_pre, query_all)
        + project_back(dkey_pre, key_all)
        + project_back(dvalue_pre, value_all)
    )
    slice_width = checkpoint.shape[1]
    x_own = checkpoint.astype(jnp.float32)
    gain_own = norm_gain.astype(jnp.float32)
    input_full = lax.psum(partial_input.astype(jnp.bfloat16), "tensor").astype(jnp.float32)
    row_sum = jnp.sum(gain_wide * input_full * x_wide, -1, keepdims=True)
    input_own = lax.dynamic_slice_in_dim(
        input_full, lax.axis_index("tensor") * slice_width, slice_width, 1
    )
    d_checkpoint = (
        inverse * gain_own * input_own - x_own * inverse**3 * row_sum / model_width
    ).astype(jnp.bfloat16)
    grad_gain = lax.psum(jnp.sum(input_own * x_own * inverse, 0), "dp")
    token_grads = jnp.concatenate([dquery_pre, dkey_pre, dvalue_pre], 1)
    own_rows = w_query.shape[0]
    feature_cols = lax.all_to_all(normed, "dp", split_axis=1, concat_axis=0, tiled=True)
    piece = lax.all_gather(token_grads, "dp", axis=0, tiled=True)
    piece_rows = piece.shape[0]
    blocks = piece_rows // row_count
    block_x = feature_cols.reshape(blocks, row_count, own_rows)
    block_g = piece.reshape(blocks, row_count, piece.shape[1])
    terms = jnp.einsum("btd,btc->bdc", block_x, block_g, preferred_element_type=jnp.float32)
    weight_grads = jnp.sum(round_half(terms).astype(jnp.float32), 0)
    query_cols = w_query.shape[1]
    key_cols = w_key.shape[1]
    grad_query = weight_grads[:, :query_cols]
    grad_key = weight_grads[:, query_cols : query_cols + key_cols]
    grad_value = weight_grads[:, query_cols + key_cols :]
    return (d_checkpoint, grad_gain, grad_query, grad_key, grad_value)


def solution(mesh):
    return jax.shard_map(
        on_device,
        mesh=mesh,
        in_specs=(
            P(("sweep", "dp"), "tensor"),
            P(("sweep", "tensor")),
            P(("sweep", "dp"), "tensor"),
            P(("sweep", "dp"), "tensor"),
            P(("sweep", "dp"), "tensor"),
            P(("sweep", "dp"), "tensor"),
        ),
        out_specs=(
            P(("sweep", "dp"), "tensor"),
            P(("sweep", "tensor")),
            P(("sweep", "dp"), "tensor"),
            P(("sweep", "dp"), "tensor"),
            P(("sweep", "dp"), "tensor"),
        ),
        check_vma=False,
    )
```

profile of v0, /device:TPU:0, one launch (start us, length us, event | category | flops | bytes accessed | tf_op | source)
XLA Modules:
  0.0 710.5 jit_solution(5812037475579603408)
XLA Ops:
  10.0 6.4 all_gather.31
  18.0 16.9 %all-gather.7.cloned.1.call-done = bf16[128,8192]{1,0:T(8,128)(2,1)} async-done(((bf16[128,2048]{1,0:T(8,128)(2,1)}), bf16[128,8192]{1,0:T(8,128)(2,1)}) %all-gather.7.cloned.1.call-update) | async-done | bytes 2097168 | tf_op jit(solution)/shard_map/all_gather | solution.py:58
  39.1 47.0 %all-gather.13.cloned.1.call-done = bf16[8192,128]{1,0:T(8,128)(2,1)} async-done(((bf16[1024,128]{1,0:T(8,128)(2,1)}), bf16[8192,128]{1,0:T(8,128)(2,1)}) %all-gather.13.cloned.1.call-update) | async-done | bytes 2097168 | tf_op jit(solution)/shard_map/all_gather | solution.py:69
  88.4 5.4 all_gather.37
  94.2 41.7 %all-gather.9.cloned.1.call-done = bf16[8192,128]{1,0:T(8,128)(2,1)} async-done(((bf16[1024,128]{1,0:T(8,128)(2,1)}), bf16[8192,128]{1,0:T(8,128)(2,1)}) %all-gather.9.cloned.1.call-update) | async-done | bytes 2097168 | tf_op jit(solution)/shard_map/all_gather | solution.py:68
  138.2 5.8 all_gather.33
  144.7 32.5 %all_gather.34 = bf16[1024,128]{1,0:T(8,128)(2,1)S(1)} all-gather(bf16[128,128]{1,0:T(8,128)(2,1)S(1)} %pad_maximum_fusion.6), channel_id=1, replica_groups=mesh['sweep'=1,'dp'=8,'tensor'=4] {'dp'}, dimensions={0}, use_global_device_ids=true | all-gather | bytes 294912 | tf_op jit(solution)/shard_map/all_gather | solution.py:103
  177.2 34.9 %all-gather = bf16[1024,128,1]{1,0,2:T(8,128)(2,1)} all-gather(bf16[128,128,1]{1,0,2:T(8,128)(2,1)S(1)} %copy.84), channel_id=2, replica_groups=mesh['sweep'=1,'dp'=8,'tensor'=4] {'dp'}, dimensions={0}, use_global_device_ids=true | all-gather | bytes 294912 | tf_op jit(solution)/shard_map/all_gather | solution.py:104
  212.1 155.9 %all-gather.11.cloned.1.call-done = bf16[8192,1024]{1,0:T(8,128)(2,1)} async-done(((bf16[1024,1024]{1,0:T(8,128)(2,1)}), bf16[8192,1024]{1,0:T(8,128)(2,1)}) %all-gather.11.cloned.1.call-update) | async-done | bytes 16777232 | tf_op jit(solution)/shard_map/all_gather | solution.py:67
  368.0 8.1 %convolution_bitcast_fusion = f32[16,8,8,128]{3,1,2,0:T(8,128)S(1)} fusion(bf16[128,8192]{1,0:T(8,128)(2,1)S(1)} %fusion.3, bf16[8192,1024]{1,0:T(8,128)(2,1)} %all-gather.11.cloned.1.call-done), kind=kOutput, calls=%fused_computation.37 | convolution fusion | flops 2147483648 | bytes 19398656 | tf_op jit(solution)/shard_map/dot_general | solution.py:75
  391.2 56.3 %reduce-scatter.5.cloned.1.call-done = bf16[128,128]{1,0:T(8,128)(2,1)} async-done(((bf16[1024,128]{1,0:T(8,128)(2,1)}), bf16[128,128]{1,0:T(8,128)(2,1)}) %reduce-scatter.5.cloned.1.call-update) | async-done | bytes 32784 | tf_op jit(solution)/shard_map/reduce_scatter | solution.py:143
  451.3 13.5 %fusion.91 = f32[128,8192]{1,0:T(8,128)} fusion(bf16[128,1024]{0,1:T(8,128)(2,1)S(1)} %bitcast.168, bf16[8192,1024]{1,0:T(8,128)(2,1)} %all-gather.11.cloned.1.call-done), kind=kOutput, calls=%fused_computation.102 | convolution fusion | flops 2147483648 | bytes 21233664 | tf_op jit(solution)/shard_map/tc,dc->td/dot_general | solution.py:50
  464.8 47.7 %reduce-scatter.9.cloned.1.call-done = bf16[128,128]{1,0:T(8,128)(2,1)} async-done(((bf16[1024,128]{1,0:T(8,128)(2,1)}), bf16[128,128]{1,0:T(8,128)(2,1)}) %reduce-scatter.9.cloned.1.call-update) | async-done | bytes 32784 | tf_op jit(solution)/shard_map/reduce_scatter | solution.py:149
  515.6 18.7 %reduce-scatter.7.cloned.1.call-done = bf16[128,128]{0,1:T(8,128)(2,1)} async-done(((bf16[128,512]{0,1:T(8,128)(2,1)}), bf16[128,128]{0,1:T(8,128)(2,1)}) %reduce-scatter.7.cloned.1.call-update) | async-done | bytes 32784 | tf_op jit(solution)/shard_map/reduce_scatter | solution.py:171
  534.2 5.6 convolution_add_fusion.1
  539.8 17.1 %reduce-scatter.11.cloned.1.call-done = bf16[128,128]{0,1:T(8,128)(2,1)} async-done(((bf16[128,512]{0,1:T(8,128)(2,1)}), bf16[128,128]{0,1:T(8,128)(2,1)}) %reduce-scatter.11.cloned.1.call-update) | async-done | bytes 32784 | tf_op jit(solution)/shard_map/reduce_scatter | solution.py:174
  556.9 4.9 fusion
  565.2 5.5 all-to-all-start
  570.7 42.7 %all-reduce.2.cloned.1.call-done = bf16[128,8192]{1,0:T(8,128)(2,1)} async-done(((bf16[128,8192]{1,0:T(8,128)(2,1)}), bf16[128,8192]{1,0:T(8,128)(2,1)}) %all-reduce.2.cloned.1.call-update) | async-done | bytes 2097168 | tf_op jit(solution)/shard_map/psum | solution.py:193
  617.8 23.2 %psum.15 = f32[2048]{0:T(1024)} all-reduce(f32[2048]{0:T(1024)S(1)} %get-tuple-element.7), channel_id=1, replica_groups=mesh['sweep'=1,'dp'=8,'tensor'=4] {'dp'}, use_global_device_ids=true, to_apply=%region_11.12 | all-reduce | flops 2048 | bytes 16384 | tf_op jit(solution)/shard_map/psum | solution.py:201
  641.0 31.3 %all-gather.15.cloned.1.call-done = bf16[1024,1280]{0,1:T(8,128)(2,1)} async-done(((bf16[128,1280]{0,1:T(8,128)(2,1)}), bf16[1024,1280]{0,1:T(8,128)(2,1)}) %all-gather.15.cloned.1.call-update) | async-done | bytes 2621456 | tf_op jit(solution)/shard_map/all_gather | solution.py:205
  672.4 4.4 copy.69
  676.7 11.9 %convolution_convert_fusion = bf16[8,1024,1280]{2,1,0:T(8,128)(2,1)} fusion(bf16[8,128,1280]{2,1,0:T(8,128)(2,1)} %bitcast.165, bf16[128,8,1024]{0,2,1:T(8,128)(2,1)} %all-to-all-done), kind=kOutput, calls=%fused_computation.1 | convolution fusion | flops 2694840320 | bytes 25690112 | tf_op jit(solution)/shard_map/btd,btc->bdc/dot_general | solution.py:210
  688.7 11.3 %convert_reduce_fusion = f32[1024,1280]{1,0:T(8,128)S(1)} fusion(bf16[8,1024,1280]{2,1,0:T(8,128)(2,1)} %convolution_convert_fusion), kind=kLoop, calls=%fused_computation | loop fusion | flops 19660800 | bytes 26214400 | tf_op jit(solution)/shard_map/reduce_sum | solution.py:211
  (95 shorter events, 47.2 us)
Async XLA Ops:
  7.2 27.7 %all-gather.7.cloned.1.call-start = ((), (), s32[]{:S(2)}) async-start(), calls=%async_computation.5 | async-start | bytes 2621440 | tf_op jit(solution)/shard_map/all_gather | solution.py:58
  7.9 78.2 %all-gather.13.cloned.1.call-start = ((), (), s32[]{:S(2)}) async-start(), calls=%async_computation.8 | async-start | bytes 2359296 | tf_op jit(solution)/shard_map/all_gather | solution.py:69
  8.6 127.2 %all-gather.9.cloned.1.call-start = ((), (), s32[]{:S(2)}) async-start(), calls=%async_computation.6 | async-start | bytes 2359296 | tf_op jit(solution)/shard_map/all_gather | solution.py:68
  9.4 358.6 %all-gather.11.cloned.1.call-start = ((), (), s32[]{:S(2)}) async-start(), calls=%async_computation.7 | async-start | bytes 18874368 | tf_op jit(solution)/shard_map/all_gather | solution.py:67
  10.0 437.6 %reduce-scatter.5.cloned.1.call-start = ((), (), s32[]{:S(2)}) async-start(), calls=%async_computation.9 | async-start | bytes 294912 | tf_op jit(solution)/shard_map/reduce_scatter | solution.py:143
  376.6 1.7 copy-start.8
  377.4 2.2 copy-start.1
  378.3 1.3 copy-start.7
  381.1 1.3 copy-start.4
  387.1 125.4 %reduce-scatter.9.cloned.1.call-start = ((), (), s32[]{:S(2)}) async-start(), calls=%async_computation.11 | async-start | bytes 294912 | tf_op jit(solution)/shard_map/reduce_scatter | solution.py:149
  391.2 143.0 %reduce-scatter.7.cloned.1.call-start = ((), (), s32[]{:S(2)}) async-start(), calls=%async_computation.10 | async-start | bytes 163840 | tf_op jit(solution)/shard_map/reduce_scatter | solution.py:171
  450.3 0.7 copy-start.6
  451.0 105.9 %reduce-scatter.11.cloned.1.call-start = ((), (), s32[]{:S(2)}) async-start(), calls=%async_computation.12 | async-start | bytes 163840 | tf_op jit(solution)/shard_map/reduce_scatter | solution.py:174
  514.8 0.7 copy-start.5
  515.5 97.9 %all-reduce.2.cloned.1.call-start = ((), (), s32[]{:S(2)}) async-start(), calls=%async_computation.13 | async-start | bytes 4194304 | tf_op jit(solution)/shard_map/psum | solution.py:193
  539.8 22.1 %copy-start.9 = (bf16[128,128]{0,1:T(8,128)(2,1)S(1)}, bf16[128,128]{0,1:T(8,128)(2,1)}, u32[]{:S(2)}) copy-start(bf16[128,128]{0,1:T(8,128)(2,1)} %reduce-scatter.7.cloned.1.call-done) | copy-start | bytes 98308
  556.9 5.0 copy-start.10
  561.9 110.5 %all-gather.15.cloned.1.call-start = ((), (), s32[]{:S(2)}) async-start(), calls=%async_computation.14 | async-start | bytes 2949120 | tf_op jit(solution)/shard_map/all_gather | solution.py:205
  562.7 8.0 %copy-start.11 = (bf16[2048]{0:T(1024)(128)(2,1)S(1)}, bf16[2048]{0:T(1024)(128)(2,1)}, u32[]{:S(2)}) copy-start(bf16[2048]{0:T(1024)(128)(2,1)} %param.7) | copy-start | bytes 12292
  565.2 111.6 %all-to-all-start = ((bf16[128,8,1024]{0,2,1:T(8,128)(2,1)}), bf16[128,8,1024]{0,2,1:T(8,128)(2,1)}, u32[]{:S(2)}, u32[]{:S(2)}) async-start(bf16[128,8,1024]{0,2,1:T(8,128)(2,1)} %bitcast.166), calls=%async_computation.4 | async-start | bytes 4194304 | tf_op jit(solution)/shard_map/all_to_all | solution.py:204
  570.7 44.9 %copy-start = (bf16[128,8192]{1,0:T(8,128)(2,1)S(1)}, bf16[128,8192]{1,0:T(8,128)(2,1)}, u32[]{:S(2)}) copy-start(bf16[128,8192]{1,0:T(8,128)(2,1)} %all-gather.7.cloned.1.call-done) | copy-start | bytes 6291460
  570.7 45.7 %copy-start.3 = (bf16[128,2048]{1,0:T(8,128)(2,1)S(1)}, bf16[128,2048]{1,0:T(8,128)(2,1)}, u32[]{:S(2)}) copy-start(bf16[128,2048]{1,0:T(8,128)(2,1)} %param.6) | copy-start | bytes 1572868
  613.4 2.2 copy-start.2
Sparse Core Ops, SparseCore 0:
  9.5 25.2 all-gather.6
  37.0 49.0 all-gather.12
  88.2 47.6 all-gather.8
  137.9 230.0 all-gather.10
  387.2 60.2 reduce-scatter.4
  451.3 61.1 reduce-scatter.8
  515.5 18.7 reduce-scatter.6
  537.2 19.6 reduce-scatter.10
  562.0 51.3 all-reduce.1
  615.9 56.4 all-gather.14
where the time goes:
time: 711 us; the launch traced here: 710 us
  waiting for transfers between devices  478 us (67%)
  blocking collectives  108 us (15%)
  matrix products  60.2 us (8%)
  other arithmetic  24.1 us (3%)
  local copies, waits for them, and re-layouts  19.3 us (3%)
  between operations  14.6 us (2%)
    all_gather x1, waiting for transfers between devices, on_device(): lax.all_gather(w_query, 'dp', axis=0, tiled=True)  156 us
    reduce_scatter x1, waiting for transfers between devices, on_device(): lax.psum_scatter(dkey_part.reshape(seq_length, own_kv * head_width).astyp...  56.3 us
    reduce_scatter x1, waiting for transfers between devices, on_device(): lax.psum_scatter(dvalue_part.reshape(seq_length, own_kv * head_width).ast...  47.7 us
    all_gather x1, waiting for transfers between devices, on_device(): lax.all_gather(w_value, 'dp', axis=0, tiled=True)  47 us
    psum x1, waiting for transfers between devices, on_device(): lax.psum(partial_input.astype(jnp.bfloat16), 'tensor').astype(jnp.float32)  42.7 us
    all_gather x1, waiting for transfers between devices, on_device(): lax.all_gather(w_key, 'dp', axis=0, tiled=True)  41.7 us
    all_gather x1, blocking collectives, on_device(): lax.all_gather(value_half, 'dp', axis=0, tiled=True)  34.9 us
    all_gather x1, blocking collectives, on_device(): lax.all_gather(key_rot, 'dp', axis=0, tiled=True)  32.5 us
  transfers between devices with their start and end apart: 11, of which 10 were waited for; matrix products, arithmetic and copies ran while one was open for 7% of the time, Pallas kernels for 0%

commit v1 on v0

--- a/solution.py
+++ b/solution.py
@@ -190,7 +190,9 @@
     slice_width = checkpoint.shape[1]
     x_own = checkpoint.astype(jnp.float32)
     gain_own = norm_gain.astype(jnp.float32)
-    input_full = lax.psum(partial_input.astype(jnp.bfloat16), "tensor").astype(jnp.float32)
+    input_full = jnp.sum(
+        lax.all_gather(partial_input.astype(jnp.bfloat16), "tensor"), axis=0
+    ).astype(jnp.float32)
     row_sum = jnp.sum(gain_wide * input_full * x_wide, -1, keepdims=True)
     input_own = lax.dynamic_slice_in_dim(
         input_full, lax.axis_index("tensor") * slice_width, slice_width, 1

time: 711 us -> 738 us (1.038)
  waiting for transfers between devices: 478 us -> 503 us
    psum x1 -> x0, waiting for transfers between devices: 42.7 us -> none  [on_device(): lax.psum(partial_input.astype(jnp.bfloat16), 'tensor').astype(jnp.float32)]
    all_gather x1, waiting for transfers between devices: 31.3 us -> 62.2 us  [on_device(): piece = lax.all_gather(token_grads, 'dp', axis=0, tiled=True)]
    all_gather x0 -> x1, waiting for transfers between devices: none -> 23.2 us  [on_device(): lax.all_gather(partial_input.astype(jnp.bfloat16), 'tensor')]
  transfers between devices with their start and end apart: 11 -> 11, of which waited for: 10 -> 11; matrix products, arithmetic and copies ran while one was open for 7% -> 11% of each run, Pallas kernels for 0% -> 0%
where the time goes in v1:
time: 738 us; the launch traced here: 737 us
  waiting for transfers between devices  503 us (68%)
  blocking collectives  107 us (14%)
  matrix products  55.9 us (8%)
  other arithmetic  29.5 us (4%)
  local copies, waits for them, and re-layouts  20.9 us (3%)
  between operations  14.7 us (2%)
    all_gather x1, waiting for transfers between devices, on_device(): lax.all_gather(w_query, 'dp', axis=0, tiled=True)  156 us
    all_gather x1, waiting for transfers between devices, on_device(): piece = lax.all_gather(token_grads, 'dp', axis=0, tiled=True)  62.2 us
    reduce_scatter x1, waiting for transfers between devices, on_device(): lax.psum_scatter(dkey_part.reshape(seq_length, own_kv * head_width).astyp...  61.8 us
    reduce_scatter x1, waiting for transfers between devices, on_device(): lax.psum_scatter(dvalue_part.reshape(seq_length, own_kv * head_width).ast...  49.6 us
    all_gather x1, waiting for transfers between devices, on_device(): lax.all_gather(w_value, 'dp', axis=0, tiled=True)  46.5 us
    all_gather x1, waiting for transfers between devices, on_device(): lax.all_gather(w_key, 'dp', axis=0, tiled=True)  41.7 us
    all_gather x1, blocking collectives, on_device(): lax.all_gather(value_half, 'dp', axis=0, tiled=True)  34.7 us
    all_gather x1, blocking collectives, on_device(): lax.all_gather(key_rot, 'dp', axis=0, tiled=True)  32.5 us
  transfers between devices with their start and end apart: 11, of which 11 were waited for; matrix products, arithmetic and copies ran while one was open for 11% of the time, Pallas kernels for 0%

profile of v1, /device:TPU:0, one launch (start us, length us, event | category | flops | bytes accessed | tf_op | source)
XLA Modules:
  0.0 737.2 jit_solution(17070906995359006764)
XLA Ops:
  10.0 6.4 all_gather.37
  19.4 15.5 %all-gather.9.cloned.1.call-done = bf16[128,8192]{1,0:T(8,128)(2,1)} async-done(((bf16[128,2048]{1,0:T(8,128)(2,1)}), bf16[128,8192]{1,0:T(8,128)(2,1)}) %all-gather.9.cloned.1.call-update) | async-done | bytes 2097168 | tf_op jit(solution)/shard_map/all_gather | solution.py:58
  39.6 46.5 %all-gather.15.cloned.1.call-done = bf16[8192,128]{1,0:T(8,128)(2,1)} async-done(((bf16[1024,128]{1,0:T(8,128)(2,1)}), bf16[8192,128]{1,0:T(8,128)(2,1)}) %all-gather.15.cloned.1.call-update) | async-done | bytes 2097168 | tf_op jit(solution)/shard_map/all_gather | solution.py:69
  88.4 5.4 all_gather.43
  94.2 41.7 %all-gather.11.cloned.1.call-done = bf16[8192,128]{1,0:T(8,128)(2,1)} async-done(((bf16[1024,128]{1,0:T(8,128)(2,1)}), bf16[8192,128]{1,0:T(8,128)(2,1)}) %all-gather.11.cloned.1.call-update) | async-done | bytes 2097168 | tf_op jit(solution)/shard_map/all_gather | solution.py:68
  138.2 5.8 all_gather.39
  144.7 32.5 %all_gather.40 = bf16[1024,128]{1,0:T(8,128)(2,1)S(1)} all-gather(bf16[128,128]{1,0:T(8,128)(2,1)S(1)} %pad_maximum_fusion.6), channel_id=1, replica_groups=mesh['sweep'=1,'dp'=8,'tensor'=4] {'dp'}, dimensions={0}, use_global_device_ids=true | all-gather | bytes 294912 | tf_op jit(solution)/shard_map/all_gather | solution.py:103
  177.2 34.7 %all-gather = bf16[1024,128,1]{1,0,2:T(8,128)(2,1)} all-gather(bf16[128,128,1]{1,0,2:T(8,128)(2,1)S(1)} %copy.83), channel_id=2, replica_groups=mesh['sweep'=1,'dp'=8,'tensor'=4] {'dp'}, dimensions={0}, use_global_device_ids=true | all-gather | bytes 294912 | tf_op jit(solution)/shard_map/all_gather | solution.py:104
  211.9 156.1 %all-gather.13.cloned.1.call-done = bf16[8192,1024]{1,0:T(8,128)(2,1)} async-done(((bf16[1024,1024]{1,0:T(8,128)(2,1)}), bf16[8192,1024]{1,0:T(8,128)(2,1)}) %all-gather.13.cloned.1.call-update) | async-done | bytes 16777232 | tf_op jit(solution)/shard_map/all_gather | solution.py:67
  368.0 8.1 %convolution_bitcast_fusion = f32[16,8,8,128]{3,1,2,0:T(8,128)S(1)} fusion(bf16[128,8192]{1,0:T(8,128)(2,1)S(1)} %fusion.3, bf16[8192,1024]{1,0:T(8,128)(2,1)} %all-gather.13.cloned.1.call-done), kind=kOutput, calls=%fused_computation.37 | convolution fusion | flops 2147483648 | bytes 19398656 | tf_op jit(solution)/shard_map/dot_general | solution.py:75
  381.6 3.7 fusion.47
  392.3 49.6 %reduce-scatter.9.cloned.1.call-done = bf16[128,128]{1,0:T(8,128)(2,1)} async-done(((bf16[1024,128]{1,0:T(8,128)(2,1)}), bf16[128,128]{1,0:T(8,128)(2,1)}) %reduce-scatter.9.cloned.1.call-update) | async-done | bytes 32784 | tf_op jit(solution)/shard_map/reduce_scatter | solution.py:149
  444.9 61.8 %reduce-scatter.5.cloned.1.call-done = bf16[128,128]{1,0:T(8,128)(2,1)} async-done(((bf16[1024,128]{1,0:T(8,128)(2,1)}), bf16[128,128]{1,0:T(8,128)(2,1)}) %reduce-scatter.5.cloned.1.call-update) | async-done | bytes 32784 | tf_op jit(solution)/shard_map/reduce_scatter | solution.py:143
  510.9 17.6 %reduce-scatter.11.cloned.1.call-done = bf16[128,128]{0,1:T(8,128)(2,1)} async-done(((bf16[128,512]{0,1:T(8,128)(2,1)}), bf16[128,128]{0,1:T(8,128)(2,1)}) %reduce-scatter.11.cloned.1.call-update) | async-done | bytes 32784 | tf_op jit(solution)/shard_map/reduce_scatter | solution.py:174
  528.4 22.7 %reduce-scatter.7.cloned.1.call-done = bf16[128,128]{0,1:T(8,128)(2,1)} async-done(((bf16[128,512]{0,1:T(8,128)(2,1)}), bf16[128,128]{0,1:T(8,128)(2,1)}) %reduce-scatter.7.cloned.1.call-update) | async-done | bytes 32784 | tf_op jit(solution)/shard_map/reduce_scatter | solution.py:171
  552.7 13.5 %fusion.91 = f32[128,8192]{1,0:T(8,128)} fusion(bf16[128,1024]{0,1:T(8,128)(2,1)S(1)} %bitcast.171, bf16[8192,1024]{1,0:T(8,128)(2,1)} %all-gather.13.cloned.1.call-done), kind=kOutput, calls=%fused_computation.102 | convolution fusion | flops 2147483648 | bytes 21233664 | tf_op jit(solution)/shard_map/tc,dc->td/dot_general | solution.py:50
  566.2 3.7 convolution_add_fusion.1
  574.5 5.5 all-to-all-start
  580.1 62.2 %all-gather.17.cloned.1.call-done = bf16[1024,1280]{0,1:T(8,128)(2,1)} async-done(((bf16[128,1280]{0,1:T(8,128)(2,1)}), bf16[1024,1280]{0,1:T(8,128)(2,1)}) %all-gather.17.cloned.1.call-update) | async-done | bytes 2621456 | tf_op jit(solution)/shard_map/all_gather | solution.py:207
  648.9 12.1 %convolution_convert_fusion = bf16[8,1024,1280]{2,1,0:T(8,128)(2,1)} fusion(bf16[8,128,1280]{2,1,0:T(8,128)(2,1)S(1)} %bitcast.166, bf16[128,8,1024]{0,2,1:T(8,128)(2,1)} %all-to-all-done), kind=kOutput, calls=%fused_computation.1 | convolution fusion | flops 2694840320 | bytes 25690112 | tf_op jit(solution)/shard_map/btd,btc->bdc/dot_general | solution.py:212
  661.0 11.4 %convert_reduce_fusion = f32[1024,1280]{1,0:T(8,128)S(1)} fusion(bf16[8,1024,1280]{2,1,0:T(8,128)(2,1)} %convolution_convert_fusion), kind=kLoop, calls=%fused_computation | loop fusion | flops 19660800 | bytes 26214400 | tf_op jit(solution)/shard_map/reduce_sum | solution.py:213
  676.1 23.2 %all-gather.19.cloned.1.call-done = bf16[512,8192]{1,0:T(8,128)(2,1)} async-done(((bf16[128,8192]{1,0:T(8,128)(2,1)}), bf16[512,8192]{1,0:T(8,128)(2,1)}) %all-gather.19.cloned.1.call-update) | async-done | bytes 8388624 | tf_op jit(solution)/shard_map/all_gather | solution.py:194
  699.3 5.1 reduce_sum.72
  708.2 22.2 %psum.7 = f32[2048]{0:T(1024)} all-reduce(f32[2048]{0:T(1024)S(1)} %get-tuple-element.7), channel_id=1, replica_groups=mesh['sweep'=1,'dp'=8,'tensor'=4] {'dp'}, use_global_device_ids=true, to_apply=%region_11.12 | all-reduce | flops 2048 | bytes 16384 | tf_op jit(solution)/shard_map/psum | solution.py:203
  (120 shorter events, 55.6 us)
Async XLA Ops:
  7.2 27.7 %all-gather.9.cloned.1.call-start = ((), (), s32[]{:S(2)}) async-start(), calls=%async_computation.5 | async-start | bytes 2621440 | tf_op jit(solution)/shard_map/all_gather | solution.py:58
  7.9 78.2 %all-gather.15.cloned.1.call-start = ((), (), s32[]{:S(2)}) async-start(), calls=%async_computation.8 | async-start | bytes 2359296 | tf_op jit(solution)/shard_map/all_gather | solution.py:69
  8.6 127.2 %all-gather.11.cloned.1.call-start = ((), (), s32[]{:S(2)}) async-start(), calls=%async_computation.6 | async-start | bytes 2359296 | tf_op jit(solution)/shard_map/all_gather | solution.py:68
  9.4 358.6 %all-gather.13.cloned.1.call-start = ((), (), s32[]{:S(2)}) async-start(), calls=%async_computation.7 | async-start | bytes 18874368 | tf_op jit(solution)/shard_map/all_gather | solution.py:67
  10.0 431.9 %reduce-scatter.9.cloned.1.call-start = ((), (), s32[]{:S(2)}) async-start(), calls=%async_computation.11 | async-start | bytes 294912 | tf_op jit(solution)/shard_map/reduce_scatter | solution.py:149
  16.4 69.7 %copy-start.13 = (f32[8192]{0:T(1024)}, f32[8192]{0:T(1024)S(1)}, u32[]{:S(2)}) copy-start(f32[8192]{0:T(1024)S(1)} %convert_element_type.122) | copy-start | bytes 98308
  37.5 50.9 %copy-start.21 = (f32[128]{0:T(128)}, f32[128]{0:T(128)S(1)}, u32[]{:S(2)}) copy-start(f32[128]{0:T(128)S(1)} %get-tuple-element.22) | copy-start | bytes 1540
  368.0 8.4 %copy-start.6 = (f32[128,64]{1,0:T(8,128)S(1)}, f32[128,64]{1,0:T(8,128)}, u32[]{:S(2)}) copy-start(f32[128,64]{1,0:T(8,128)} %get-tuple-element.19) | copy-start | bytes 98308
  368.0 8.5 %copy-start.8 = (f32[128,64]{1,0:T(8,128)S(1)}, f32[128,64]{1,0:T(8,128)}, u32[]{:S(2)}) copy-start(f32[128,64]{1,0:T(8,128)} %get-tuple-element.20) | copy-start | bytes 98308
  381.4 125.4 %reduce-scatter.5.cloned.1.call-start = ((), (), s32[]{:S(2)}) async-start(), calls=%async_computation.9 | async-start | bytes 294912 | tf_op jit(solution)/shard_map/reduce_scatter | solution.py:143
  381.6 3.7 copy-start.2
  381.6 3.7 copy-start.16
  381.6 3.7 copy-start.17
  388.2 122.1 %copy-start.7 = (f32[128,64]{1,0:T(8,128)S(1)}, f32[128,64]{1,0:T(8,128)}, u32[]{:S(2)}) copy-start(f32[128,64]{1,0:T(8,128)} %get-tuple-element.19) | copy-start | bytes 98308
  388.2 122.1 %copy-start.9 = (f32[128,64]{1,0:T(8,128)S(1)}, f32[128,64]{1,0:T(8,128)}, u32[]{:S(2)}) copy-start(f32[128,64]{1,0:T(8,128)} %get-tuple-element.20) | copy-start | bytes 98308
  389.7 138.8 %reduce-scatter.11.cloned.1.call-start = ((), (), s32[]{:S(2)}) async-start(), calls=%async_computation.12 | async-start | bytes 163840 | tf_op jit(solution)/shard_map/reduce_scatter | solution.py:174
  444.9 106.2 %reduce-scatter.7.cloned.1.call-start = ((), (), s32[]{:S(2)}) async-start(), calls=%async_computation.10 | async-start | bytes 163840 | tf_op jit(solution)/shard_map/reduce_scatter | solution.py:171
  510.2 132.1 %all-gather.17.cloned.1.call-start = ((), (), s32[]{:S(2)}) async-start(), calls=%async_computation.13 | async-start | bytes 2949120 | tf_op jit(solution)/shard_map/all_gather | solution.py:207
  552.7 13.6 %copy-start.19 = (bf16[128,128]{0,1:T(8,128)(2,1)S(1)}, bf16[128,128]{0,1:T(8,128)(2,1)}, u32[]{:S(2)}) copy-start(bf16[128,128]{0,1:T(8,128)(2,1)} %reduce-scatter.7.cloned.1.call-done) | copy-start | bytes 98308
  552.7 146.6 %all-gather.19.cloned.1.call-start = ((), (), s32[]{:S(2)}) async-start(), calls=%async_computation.14 | async-start | bytes 10485760 | tf_op jit(solution)/shard_map/all_gather | solution.py:194
  566.2 3.7 copy-start.3
  566.2 3.7 copy-start.18
  572.0 8.0 %copy-start.20 = (bf16[2048]{0:T(1024)(128)(2,1)S(1)}, bf16[2048]{0:T(1024)(128)(2,1)}, u32[]{:S(2)}) copy-start(bf16[2048]{0:T(1024)(128)(2,1)} %param.7) | copy-start | bytes 12292
  574.5 74.4 %all-to-all-start = ((bf16[128,8,1024]{0,2,1:T(8,128)(2,1)}), bf16[128,8,1024]{0,2,1:T(8,128)(2,1)}, u32[]{:S(2)}, u32[]{:S(2)}) async-start(bf16[128,8,1024]{0,2,1:T(8,128)(2,1)} %bitcast.168), calls=%async_computation.4 | async-start | bytes 4194304 | tf_op jit(solution)/shard_map/all_to_all | solution.py:206
  (11 other events, 19.8 us)
Sparse Core Ops, SparseCore 0:
  9.5 25.2 all-gather.8
  37.0 49.0 all-gather.14
  88.2 47.6 all-gather.10
  137.9 230.0 all-gather.12
  381.5 60.3 reduce-scatter.8
  445.6 61.0 reduce-scatter.4
  509.7 18.6 reduce-scatter.10
  531.4 19.6 reduce-scatter.6
  553.7 88.4 all-gather.16
  643.7 55.5 all-gather.18
